TPU v7x, 512 devices: a 8x2x16 block of a 8x8x16 slice. The times are simulated.
512 devices in a mesh: group: 2 (over y), ha: 16 (over x, core), wa: 16 (over z).
Axes of the slice: x: 8, y: 2, z: 16, core: 2. Of those that a mesh axis runs over, the one named last changes fastest.
The devices are a block of a 8x8x16 slice.
Arguments:
- queries: bfloat16 [4, 128, 128, 1536], P('group', 'ha', 'wa'), parts along dimension 0, may hold values from -6 to 6
- keys: bfloat16 [4, 128, 128, 1536], P('group', 'ha', 'wa'), parts along dimension 0, may hold values from -6 to 6
- values: bfloat16 [4, 128, 128, 1536], P('group', 'ha', 'wa'), parts along dimension 0, may hold values from -6 to 6
- out_grad: bfloat16 [4, 128, 128, 1536], P('group', 'ha', 'wa'), parts along dimension 0, may hold values from -96 to 96
- log_norm: float32 [12, 4, 128, 128], P(None, 'group', 'ha', 'wa'), parts along dimension 1, may hold values from 6.5 to 7.5
- delta_rows: float32 [12, 4, 128, 128], P(None, 'group', 'ha', 'wa'), parts along dimension 1, may hold values from -360 to 360
- text_keys: bfloat16 [64, 1536], P('group'), parts along dimension 0, may hold values from -6 to 6
- text_values: bfloat16 [64, 1536], P('group'), parts along dimension 0, may hold values from -6 to 6
- window_table: int32 [16, 16, 9], replicated, may hold values 0 or 1
Outputs:
- query_grad: bfloat16 [4, 128, 128, 1536], P('group', 'ha', 'wa'), parts along dimension 0
- key_grad: bfloat16 [4, 128, 128, 1536], P('group', 'ha', 'wa'), parts along dimension 0
- value_grad: bfloat16 [4, 128, 128, 1536], P('group', 'ha', 'wa'), parts along dimension 0
- text_key_grad: bfloat16 [64, 1536], P('group'), parts along dimension 0
- text_value_grad: bfloat16 [64, 1536], P('group'), parts along dimension 0
There are 2 independent parts, one for each index of `group`. A program takes and returns all parts, laid end to end along the dimension named above; an argument that names none is the same for every part. Nothing has to cross between parts.
All inputs are finite; a program needn't handle non-finite values.
Results may differ from a plain program's by a relative error of at most 0.001.
The roundings to bfloat16 on the way count: a program that leaves them out, or rounds other values in their place, can miss the bound.
Values may be sent and summed in bfloat16 or wider, within the bound.
A program may use at most 64 MiB of HBM per device.

v0:
```python
import math
import jax
import jax.numpy as jnp
from jax import lax
from jax.sharding import Mesh
from jax.sharding import PartitionSpec as P

HEADS = 12
HDIM = 128
TILE = 8
HALO = 2
HA = ("ha_0", "ha_1")
HA_WA = ("ha_0", "ha_1", "wa")


def passed_along(value, axis, steps):
    count = lax.axis_size(axis)
    pairs = [(source, (source + steps) % count) for source in range(count)]
    return lax.ppermute(value, axis, pairs)


def with_halo(cells, sides, width):
    for axis, dim in sides:
        count = lax.axis_size(axis)
        head = lax.slice_in_dim(cells, 0, width, axis=dim)
        tail = lax.slice_in_dim(cells, cells.shape[dim] - width, cells.shape[dim], axis=dim)
        cells = jnp.concatenate(
            [
                lax.ppermute(tail, axis, [(i, (i + 1) % count) for i in range(count)]),
                cells,
                lax.ppermute(head, axis, [((i + 1) % count, i) for i in range(count)]),
            ],
            axis=dim,
        )
    return cells


def one_axis_at_a_time(shard, axes):
    for axis in axes:
        shard = lax.psum(shard, axis)
    return shard


def tile_grads(query_rows, cotangent_rows, norm_rows, delta_part, key_rows, value_rows, cell_mask):
    score_scale = 1.0 / math.sqrt(query_rows.shape[-1])
    scores = (
        jnp.einsum("qhd,khd->hqk", query_rows, key_rows, preferred_element_type=jnp.float32)
        * score_scale
    )
    probs = jnp.exp(scores - norm_rows[:, :, None])
    if cell_mask is not None:
        probs = probs * cell_mask[None, None, :]
    probs_half = probs.astype(jnp.bfloat16)
    value_part = jnp.einsum(
        "hqk,qhd->khd", probs_half, cotangent_rows, preferred_element_type=jnp.float32
    )
    prob_grad = jnp.einsum(
        "qhd,khd->hqk", cotangent_rows, value_rows, preferred_element_type=jnp.float32
    )
    score_grad = (probs * (prob_grad - delta_part[:, :, None])).astype(jnp.bfloat16)
    query_part = (
        jnp.einsum("hqk,khd->qhd", score_grad, key_rows, preferred_element_type=jnp.float32)
        * score_scale
    )
    key_part = (
        jnp.einsum("hqk,qhd->khd", score_grad, query_rows, preferred_element_type=jnp.float32)
        * score_scale
    )
    return (query_part, key_part, value_part)


def send_cols(strip, offset):
    return passed_along(strip, "wa", offset)


def send_rows(strip, offset):
    return passed_along(strip, HA, offset)


def fold_band(buffer, along, mover):
    lower = lax.slice_in_dim(buffer, 0, HALO, axis=along)
    middle = lax.slice_in_dim(buffer, HALO, HALO + TILE, axis=along)
    upper = lax.slice_in_dim(buffer, HALO + TILE, TILE + 2 * HALO, axis=along)
    from_before = mover(upper, 1)
    from_after = mover(lower, -1)
    widths_low = [(0, 0)] * buffer.ndim
    widths_high = [(0, 0)] * buffer.ndim
    widths_low[along] = (0, TILE - HALO)
    widths_high[along] = (TILE - HALO, 0)
    return middle + jnp.pad(from_before, widths_low) + jnp.pad(from_after, widths_high)


def local(
    queries, keys, values, out_grad, log_norm, delta_rows, text_keys, text_values, window_table
):
    frames, tile_side, _, width = queries.shape
    window_side = TILE + 2 * HALO
    stacked = jnp.stack((keys, values))
    window = with_halo(stacked, ((HA, 2), ("wa", 3)), HALO)
    row_tile = lax.axis_index(HA)
    col_tile = lax.axis_index("wa")
    anchor = jnp.zeros((), jnp.int32)
    pattern = (
        lax.dynamic_slice(window_table, (row_tile, col_tile, anchor), (1, 1, 9))
        .reshape(3, 3)
        .astype(jnp.float32)
    )
    position = jnp.arange(window_side, dtype=jnp.int32)
    block_of = (position >= HALO).astype(jnp.int32) + (position >= HALO + TILE).astype(jnp.int32)
    one_hot = (block_of[:, None] == jnp.arange(3, dtype=jnp.int32)[None, :]).astype(jnp.float32)
    cell_grid = jnp.dot(
        jnp.dot(one_hot, pattern, precision=lax.Precision.HIGHEST),
        one_hot.T,
        precision=lax.Precision.HIGHEST,
    )
    cell_mask = jnp.broadcast_to(cell_grid[None], (frames, window_side, window_side)).reshape(-1)
    query_rows = queries.reshape(-1, HEADS, HDIM)
    cotangent_rows = out_grad.reshape(-1, HEADS, HDIM)
    norm_rows = log_norm.reshape(HEADS, -1)
    delta_part = delta_rows.reshape(HEADS, -1)
    key_rows = window[0].reshape(-1, HEADS, HDIM)
    value_rows = window[1].reshape(-1, HEADS, HDIM)
    video_query, video_key, video_value = tile_grads(
        query_rows, cotangent_rows, norm_rows, delta_part, key_rows, value_rows, cell_mask
    )
    text_query, text_key, text_value = tile_grads(
        query_rows,
        cotangent_rows,
        norm_rows,
        delta_part,
        text_keys.reshape(-1, HEADS, HDIM),
        text_values.reshape(-1, HEADS, HDIM),
        None,
    )
    query_grad = (
        (video_query + text_query).astype(jnp.bfloat16).reshape(frames, tile_side, tile_side, width)
    )
    text_total = one_axis_at_a_time(jnp.stack((text_key, text_value)), HA_WA)
    buffer = jnp.stack((video_key, video_value)).reshape(2, frames, window_side, window_side, width)
    buffer = fold_band(buffer, 3, send_cols)
    buffer = fold_band(buffer, 2, send_rows)
    text_key_grad = text_total[0].reshape(-1, width).astype(jnp.bfloat16)
    text_value_grad = text_total[1].reshape(-1, width).astype(jnp.bfloat16)
    return (
        query_grad,
        buffer[0].astype(jnp.bfloat16),
        buffer[1].astype(jnp.bfloat16),
        text_key_grad,
        text_value_grad,
    )


def solution(mesh):
    split = Mesh(
        mesh.devices.reshape(mesh.shape["group"], 8, 2, mesh.shape["wa"]),
        ("group", "ha_0", "ha_1", "wa"),
    )
    return jax.shard_map(
        local,
        mesh=split,
        in_specs=(
            P("group", HA, "wa", None),
            P("group", HA, "wa", None),
            P("group", HA, "wa", None),
            P("group", HA, "wa", None),
            P(None, "group", HA, "wa"),
            P(None, "group", HA, "wa"),
            P("group", None),
            P("group", None),
            P(),
        ),
        out_specs=(
            P("group", HA, "wa", None),
            P("group", HA, "wa", None),
            P("group", HA, "wa", None),
            P("group", None),
            P("group", None),
        ),
        check_vma=False,
    )
```

profile of v0, /device:TPU:71, one launch (start us, length us, event | category | flops | bytes accessed | tf_op | source)
XLA Modules:
  0.0 266.0 jit_solution(15022201213251635187)
XLA Ops:
  7.3 1.1 pad_maximum_fusion.7
  8.4 3.1 %collective-permute-start = (bf16[2,2,2,8,1536]{4,3,2,1,0:T(8,128)(2,1)S(1)}, bf16[2,2,2,8,1536]{4,3,2,1,0:T(8,128)(2,1)S(1)}, u32[]{:S(2)}, u32[]{:S(2)}) collective-permute-start(bf16[2,2,2,8,1536]{4,3,2,1,0:T(8,128)(2,1)S(1)} %get-tuple-element.20), channel_id=1, source_target_pairs={{0,16},{16,32},{32,48},{48,64},{64,80},{80,96},{96,112},{112,128},... | collective-permute-start | bytes 589832 | tf_op jit(solution)/shard_map/ppermute | solution.py:29
  13.3 1.3 reshape.49
  18.1 1.1 pad_maximum_fusion.5
  19.2 5.7 %collective-permute-start.2 = (bf16[2,2,12,2,1536]{4,3,2,1,0:T(2,128)(2,1)}, bf16[2,2,12,2,1536]{4,3,2,1,0:T(2,128)(2,1)S(1)}, u32[]{:S(2)}, u32[]{:S(2)}) collective-permute-start(bf16[2,2,12,2,1536]{4,3,2,1,0:T(2,128)(2,1)} %get-tuple-element.16), channel_id=1, source_target_pairs={{0,1},{1,2},{2,3},{3,4},{4,5},{5,6},{6,7},{7,8},{8,9},{9,10},{10,1... | collective-permute-start | bytes 884744 | tf_op jit(solution)/shard_map/ppermute | solution.py:29
  25.0 39.9 %collective-permute-start.3 = (bf16[2,2,12,2,1536]{4,3,2,1,0:T(2,128)(2,1)S(1)}, bf16[2,2,12,2,1536]{4,3,2,1,0:T(2,128)(2,1)S(1)}, u32[]{:S(2)}, u32[]{:S(2)}) collective-permute-start(bf16[2,2,12,2,1536]{4,3,2,1,0:T(2,128)(2,1)S(1)} %get-tuple-element.17), channel_id=1, source_target_pairs={{1,0},{2,1},{3,2},{4,3},{5,4},{6,5},{7,6},{8,7},{9,8},{10,9},{11,1... | collective-permute-start | bytes 884744 | tf_op jit(solution)/shard_map/ppermute | solution.py:31
  65.4 65.5 %all-reduce.8.cloned.1.call-done = f32[2,32,12,128]{3,1,2,0:T(8,128)} async-done(((f32[2,32,12,128]{3,1,2,0:T(8,128)}), f32[2,32,12,128]{3,1,2,0:T(8,128)}) %all-reduce.8.cloned.1.call-update) | async-done | bytes 393232 | tf_op jit(solution)/shard_map/psum | solution.py:40
  131.0 1.5 pad_maximum_fusion
  132.7 1.7 reshape_squeeze.9
  135.8 1.6 convolution_bitcast_fusion
  140.6 2.5 copy.50
  143.1 2.4 stack.30
  145.5 4.0 %copy.52 = f32[288,12,128]{2,1,0:T(8,128)} copy(f32[288,12,128]{2,0,1:T(8,128)} %convolution_bitcast_fusion) | data formatting | bytes 3538944 | tf_op jit(solution)/shard_map/hqk,qhd->khd/transpose | solution.py:54
  149.5 3.2 %stack.31 = f32[1,2,12,12,1536]{4,3,2,1,0:T(8,128)} reshape(f32[288,12,128]{2,1,0:T(8,128)} %copy.52) | data formatting | bytes 3538944 | tf_op jit(solution)/shard_map/stack | solution.py:139
  152.9 1.4 copy-done.1
  154.5 2.1 copy-done.2
  157.2 3.3 %collective-permute-start.4 = (f32[2,2,12,2,1536]{4,3,2,1,0:T(2,128)S(1)}, f32[2,2,12,2,1536]{4,3,2,1,0:T(2,128)S(1)}, u32[]{:S(2)}, u32[]{:S(2)}) collective-permute-start(f32[2,2,12,2,1536]{4,3,2,1,0:T(2,128)S(1)} %get-tuple-element.10), channel_id=1, source_target_pairs={{0,1},{1,2},{2,3},{3,4},{4,5},{5,6},{6,7},{7,8},{8,9},{9,10},{10,1... | collective-permute-start | bytes 1769480 | tf_op jit(solution)/shard_map/ppermute | solution.py:19
  160.5 5.5 %collective-permute-start.5 = (f32[2,2,12,2,1536]{4,3,2,1,0:T(2,128)S(1)}, f32[2,2,12,2,1536]{4,3,2,1,0:T(2,128)S(1)}, u32[]{:S(2)}, u32[]{:S(2)}) collective-permute-start(f32[2,2,12,2,1536]{4,3,2,1,0:T(2,128)S(1)} %get-tuple-element.11), channel_id=1, source_target_pairs={{0,15},{1,0},{2,1},{3,2},{4,3},{5,4},{6,5},{7,6},{8,7},{9,8},{10,9... | collective-permute-start | bytes 1769480 | tf_op jit(solution)/shard_map/ppermute | solution.py:19
  166.0 15.4 %all-reduce.10.cloned.1.call-done = f32[2,32,12,128]{3,1,2,0:T(8,128)} async-done(((f32[2,32,12,128]{3,1,2,0:T(8,128)}), f32[2,32,12,128]{3,1,2,0:T(8,128)}) %all-reduce.10.cloned.1.call-update) | async-done | bytes 393232 | tf_op jit(solution)/shard_map/psum | solution.py:40
  181.4 48.9 %all-reduce.11 = bf16[2,32,12,128]{3,1,2,0:T(8,128)(2,1)S(1)} all-reduce(f32[2,32,12,128]{3,1,2,0:T(8,128)} %all-reduce.10.cloned.1.call-done), channel_id=1, replica_groups=mesh['group'=2,'ha_0'=8,'ha_1'=2,'wa'=16] {'wa'}, use_global_device_ids=true, to_apply=%region_2.0 | all-reduce | flops 98304 | bytes 589824 | tf_op jit(solution)/shard_map/psum | solution.py:40
  230.4 3.0 %fusion = f32[2,2,12,8,1536]{4,3,2,1,0:T(8,128)S(1)} fusion(f32[2,2,12,12,1536]{4,3,2,1,0:T(8,128)} %copy-done.2, f32[2,2,12,2,1536]{4,3,2,1,0:T(2,128)S(1)} %collective-permute-done.5, f32[2,2,12,2,1536]{4,3,2,1,0:T(2,128)S(1)} %collective-permute-done.4), kind=kLoop, calls=%fused_computation.1 | loop fusion | flops 1179648 | bytes 5898240 | tf_op jit(solution)/shard_map/add | solution.py:90
  233.5 16.2 %collective-permute-start.6 = (f32[2,2,2,8,1536]{4,3,2,1,0:T(8,128)S(1)}, f32[2,2,2,8,1536]{4,3,2,1,0:T(8,128)S(1)}, u32[]{:S(2)}, u32[]{:S(2)}) collective-permute-start(f32[2,2,2,8,1536]{4,3,2,1,0:T(8,128)S(1)} %get-tuple-element.12), channel_id=1, source_target_pairs={{0,16},{16,32},{32,48},{48,64},{64,80},{80,96},{96,112},{112,128},... | collective-permute-start | bytes 1179656 | tf_op jit(solution)/shard_map/ppermute | solution.py:19
  250.4 4.0 %collective-permute-done.6 = f32[2,2,2,8,1536]{4,3,2,1,0:T(8,128)S(1)} collective-permute-done((f32[2,2,2,8,1536]{4,3,2,1,0:T(8,128)S(1)}, f32[2,2,2,8,1536]{4,3,2,1,0:T(8,128)S(1)}, u32[]{:S(2)}, u32[]{:S(2)}) %collective-permute-start.6) | collective-permute-done | bytes 393248 | tf_op jit(solution)/shard_map/ppermute | solution.py:19
  254.4 3.7 %collective-permute-done.7 = f32[2,2,2,8,1536]{4,3,2,1,0:T(8,128)S(1)} collective-permute-done((f32[2,2,2,8,1536]{4,3,2,1,0:T(8,128)S(1)}, f32[2,2,2,8,1536]{4,3,2,1,0:T(8,128)S(1)}, u32[]{:S(2)}, u32[]{:S(2)}) %collective-permute-start.7) | collective-permute-done | bytes 393248 | tf_op jit(solution)/shard_map/ppermute | solution.py:19
  (64 shorter events, 13.4 us)
Async XLA Ops:
  7.2 7.8 %copy-start = (bf16[32,1536]{1,0:T(8,128)(2,1)S(1)}, bf16[32,1536]{1,0:T(8,128)(2,1)}, u32[]{:S(2)}) copy-start(bf16[32,1536]{1,0:T(8,128)(2,1)} %param.15) | copy-start | bytes 294916
  7.2 7.4 %copy-start.8 = (bf16[2,8,8,1536]{3,2,1,0:T(8,128)(2,1)S(1)}, bf16[2,8,8,1536]{3,2,1,0:T(8,128)(2,1)}, u32[]{:S(2)}) copy-start(bf16[2,8,8,1536]{3,2,1,0:T(8,128)(2,1)} %param.12) | copy-start | bytes 1179652
  7.2 123.7 %all-reduce.8.cloned.1.call-start = ((), (), s32[]{:S(2)}) async-start(), calls=%async_computation | async-start | bytes 786432 | tf_op jit(solution)/shard_map/psum | solution.py:40
  7.3 8.3 %copy-start.9 = (bf16[32,1536]{1,0:T(8,128)(2,1)S(1)}, bf16[32,1536]{1,0:T(8,128)(2,1)}, u32[]{:S(2)}) copy-start(bf16[32,1536]{1,0:T(8,128)(2,1)} %param.16) | copy-start | bytes 294916
  8.4 9.7 %collective-permute-start = (bf16[2,2,2,8,1536]{4,3,2,1,0:T(8,128)(2,1)S(1)}, bf16[2,2,2,8,1536]{4,3,2,1,0:T(8,128)(2,1)S(1)}, u32[]{:S(2)}, u32[]{:S(2)}) collective-permute-start(bf16[2,2,2,8,1536]{4,3,2,1,0:T(8,128)(2,1)S(1)} %get-tuple-element.20), channel_id=1, source_target_pairs={{0,16},{16,32},{32,48},{48,64},{64,80},{80,96},{96,112},{112,128},... | collective-permute-start | bytes 589832 | tf_op jit(solution)/shard_map/ppermute | solution.py:29
  11.5 6.6 %collective-permute-start.1 = (bf16[2,2,2,8,1536]{4,3,2,1,0:T(8,128)(2,1)S(1)}, bf16[2,2,2,8,1536]{4,3,2,1,0:T(8,128)(2,1)S(1)}, u32[]{:S(2)}, u32[]{:S(2)}) collective-permute-start(bf16[2,2,2,8,1536]{4,3,2,1,0:T(8,128)(2,1)S(1)} %get-tuple-element.21), channel_id=1, source_target_pairs={{16,0},{32,16},{48,32},{64,48},{80,64},{96,80},{112,96},{128,112},... | collective-permute-start | bytes 589832 | tf_op jit(solution)/shard_map/ppermute | solution.py:31
  14.9 3.2 %copy-start.4 = (bf16[2,8,8,1536]{3,2,1,0:T(8,128)(2,1)S(1)}, bf16[2,8,8,1536]{3,2,1,0:T(8,128)(2,1)}, u32[]{:S(2)}) copy-start(bf16[2,8,8,1536]{3,2,1,0:T(8,128)(2,1)} %param.11) | copy-start | bytes 1179652
  15.0 3.2 %copy-start.5 = (bf16[2,8,8,1536]{3,2,1,0:T(8,128)(2,1)S(1)}, bf16[2,8,8,1536]{3,2,1,0:T(8,128)(2,1)}, u32[]{:S(2)}) copy-start(bf16[2,8,8,1536]{3,2,1,0:T(8,128)(2,1)} %param.10) | copy-start | bytes 1179652
  15.9 115.2 %copy-start.6 = (bf16[12,128,32]{1,2,0:T(8,128)(2,1)}, bf16[12,128,32]{1,2,0:T(8,128)(2,1)S(1)}, u32[]{:S(2)}) copy-start(bf16[12,128,32]{1,2,0:T(8,128)(2,1)S(1)} %fusion.11) | copy-start | bytes 294916
  16.9 164.4 %all-reduce.10.cloned.1.call-start = ((), (), s32[]{:S(2)}) async-start(), calls=%async_computation.1 | async-start | bytes 786432 | tf_op jit(solution)/shard_map/psum | solution.py:40
  19.2 111.8 %collective-permute-start.2 = (bf16[2,2,12,2,1536]{4,3,2,1,0:T(2,128)(2,1)}, bf16[2,2,12,2,1536]{4,3,2,1,0:T(2,128)(2,1)S(1)}, u32[]{:S(2)}, u32[]{:S(2)}) collective-permute-start(bf16[2,2,12,2,1536]{4,3,2,1,0:T(2,128)(2,1)} %get-tuple-element.16), channel_id=1, source_target_pairs={{0,1},{1,2},{2,3},{3,4},{4,5},{5,6},{6,7},{7,8},{8,9},{9,10},{10,1... | collective-permute-start | bytes 884744 | tf_op jit(solution)/shard_map/ppermute | solution.py:29
  25.0 106.0 %collective-permute-start.3 = (bf16[2,2,12,2,1536]{4,3,2,1,0:T(2,128)(2,1)S(1)}, bf16[2,2,12,2,1536]{4,3,2,1,0:T(2,128)(2,1)S(1)}, u32[]{:S(2)}, u32[]{:S(2)}) collective-permute-start(bf16[2,2,12,2,1536]{4,3,2,1,0:T(2,128)(2,1)S(1)} %get-tuple-element.17), channel_id=1, source_target_pairs={{1,0},{2,1},{3,2},{4,3},{5,4},{6,5},{7,6},{8,7},{9,8},{10,9},{11,1... | collective-permute-start | bytes 884744 | tf_op jit(solution)/shard_map/ppermute | solution.py:31
  135.8 1.6 copy-start.3
  137.9 1.0 copy-start.7
  152.7 1.7 copy-start.1
  154.5 2.1 copy-start.2
  157.2 73.2 %collective-permute-start.4 = (f32[2,2,12,2,1536]{4,3,2,1,0:T(2,128)S(1)}, f32[2,2,12,2,1536]{4,3,2,1,0:T(2,128)S(1)}, u32[]{:S(2)}, u32[]{:S(2)}) collective-permute-start(f32[2,2,12,2,1536]{4,3,2,1,0:T(2,128)S(1)} %get-tuple-element.10), channel_id=1, source_target_pairs={{0,1},{1,2},{2,3},{3,4},{4,5},{5,6},{6,7},{7,8},{8,9},{9,10},{10,1... | collective-permute-start | bytes 1769480 | tf_op jit(solution)/shard_map/ppermute | solution.py:19
  160.5 69.9 %collective-permute-start.5 = (f32[2,2,12,2,1536]{4,3,2,1,0:T(2,128)S(1)}, f32[2,2,12,2,1536]{4,3,2,1,0:T(2,128)S(1)}, u32[]{:S(2)}, u32[]{:S(2)}) collective-permute-start(f32[2,2,12,2,1536]{4,3,2,1,0:T(2,128)S(1)} %get-tuple-element.11), channel_id=1, source_target_pairs={{0,15},{1,0},{2,1},{3,2},{4,3},{5,4},{6,5},{7,6},{8,7},{9,8},{10,9... | collective-permute-start | bytes 1769480 | tf_op jit(solution)/shard_map/ppermute | solution.py:19
  233.5 20.9 %collective-permute-start.6 = (f32[2,2,2,8,1536]{4,3,2,1,0:T(8,128)S(1)}, f32[2,2,2,8,1536]{4,3,2,1,0:T(8,128)S(1)}, u32[]{:S(2)}, u32[]{:S(2)}) collective-permute-start(f32[2,2,2,8,1536]{4,3,2,1,0:T(8,128)S(1)} %get-tuple-element.12), channel_id=1, source_target_pairs={{0,16},{16,32},{32,48},{48,64},{64,80},{80,96},{96,112},{112,128},... | collective-permute-start | bytes 1179656 | tf_op jit(solution)/shard_map/ppermute | solution.py:19
  249.7 8.4 %collective-permute-start.7 = (f32[2,2,2,8,1536]{4,3,2,1,0:T(8,128)S(1)}, f32[2,2,2,8,1536]{4,3,2,1,0:T(8,128)S(1)}, u32[]{:S(2)}, u32[]{:S(2)}) collective-permute-start(f32[2,2,2,8,1536]{4,3,2,1,0:T(8,128)S(1)} %get-tuple-element.13), channel_id=1, source_target_pairs={{0,240},{16,0},{32,16},{48,32},{64,48},{80,64},{96,80},{112,96},{1... | collective-permute-start | bytes 1179656 | tf_op jit(solution)/shard_map/ppermute | solution.py:19
Sparse Core Ops, SparseCore 0:
  17.1 113.8 all-reduce.7
  133.8 47.4 all-reduce.9
where the time goes:
time: 267 us; the launch traced here: 266 us
  waiting for transfers between devices  88.7 us (33%)
  starting transfers between devices  73.8 us (28%)
  blocking collectives  48.9 us (18%)
  local copies, waits for them, and re-layouts  26 us (10%)
  between operations  14.4 us (5%)
  other arithmetic  8.7 us (3%)
  matrix products  5.43 us (2%)
    psum x2, waiting for transfers between devices, one_axis_at_a_time(): shard = lax.psum(shard, axis)  80.9 us
    psum x1, blocking collectives, one_axis_at_a_time(): shard = lax.psum(shard, axis)  48.9 us
    ppermute x2, starting transfers between devices, with_halo(): lax.ppermute(head, axis, [((i + 1) % count, i) for i in range(count)])  39.9 us
    ppermute x4, starting transfers between devices, passed_along(): return lax.ppermute(value, axis, pairs)  24.9 us
    ppermute x2, starting transfers between devices, with_halo(): lax.ppermute(tail, axis, [(i, (i + 1) % count) for i in range(count)])  8.83 us
    ppermute x4, waiting for transfers between devices, passed_along(): return lax.ppermute(value, axis, pairs)  7.7 us
    another operation x3, local copies, waits for them, and re-layouts, local(): jnp.stack((video_key, video_value))  5.77 us
  transfers between devices with their start and end apart: 10, of which 4 were waited for; matrix products, arithmetic and copies ran while one was open for 12% of the time, Pallas kernels for 0%

commit v1 on v0

--- a/solution.py
+++ b/solution.py
@@ -37,7 +37,7 @@
 
 def one_axis_at_a_time(shard, axes):
     for axis in axes:
-        shard = lax.psum(shard, axis)
+        shard = jnp.sum(lax.all_gather(shard, axis), axis=0)
     return shard
 
 

time: 267 us -> 219 us (0.82)
  the two profiles are of different devices: /device:TPU:71 before, /device:TPU:66 now
where the time goes in v1:
time: 219 us; the launch traced here: 218 us
  waiting for transfers between devices  136 us (62%)
  local copies, waits for them, and re-layouts  26.9 us (12%)
  starting transfers between devices  20.6 us (9%)
  between operations  14.4 us (7%)
  other arithmetic  12.3 us (6%)
  matrix products  5.71 us (3%)
  blocking collectives  2.42 us (1%)
    all_gather x2, waiting for transfers between devices, one_axis_at_a_time(): shard = jnp.sum(lax.all_gather(shard, axis), axis=0)  94.4 us
    ppermute x4, waiting for transfers between devices, passed_along(): return lax.ppermute(value, axis, pairs)  28.9 us
    ppermute x4, starting transfers between devices, passed_along(): return lax.ppermute(value, axis, pairs)  9.61 us
    ppermute x2, starting transfers between devices, with_halo(): lax.ppermute(head, axis, [((i + 1) % count, i) for i in range(count)])  7.08 us
    ppermute x2, waiting for transfers between devices, with_halo(): lax.ppermute(tail, axis, [(i, (i + 1) % count) for i in range(count)])  6.7 us
    reduce_sum x3, other arithmetic, one_axis_at_a_time(): shard = jnp.sum(lax.all_gather(shard, axis), axis=0)  6.66 us
    another operation x3, local copies, waits for them, and re-layouts, local(): jnp.stack((video_key, video_value))  5.85 us
    ppermute x2, waiting for transfers between devices, with_halo(): lax.ppermute(head, axis, [((i + 1) % count, i) for i in range(count)])  5.67 us
  transfers between devices with their start and end apart: 10, of which 8 were waited for; matrix products, arithmetic and copies ran while one was open for 12% of the time, Pallas kernels for 0%

profile of v1, /device:TPU:66, one launch (start us, length us, event | category | flops | bytes accessed | tf_op | source)
XLA Modules:
  0.0 218.0 jit_solution(18182901159024862926)
XLA Ops:
  14.4 84.6 %all-gather.6.cloned.1.call-done = f32[16,32,12,128]{3,1,2,0:T(8,128)} async-done(((f32[2,32,12,128]{3,1,2,0:T(8,128)}), f32[16,32,12,128]{3,1,2,0:T(8,128)}) %all-gather.6.cloned.1.call-update) | async-done | bytes 3145744 | tf_op jit(solution)/shard_map/all_gather | solution.py:40
  99.0 2.3 %reduce_sum.27 = f32[2,32,12,128]{3,1,2,0:T(8,128)S(1)} reduce(f32[8,2,32,12,128]{4,2,3,1,0:T(8,128)} %bitcast.76, f32[]{:T(128)} %constant.32.clone.1), dimensions={0}, to_apply=%region_0.0 | reduce | flops 688128 | bytes 3538948 | tf_op jit(solution)/shard_map/reduce_sum | solution.py:40
  101.3 2.4 %all-gather.1 = f32[4,32,12,128]{3,1,2,0:T(8,128)S(1)} all-gather(f32[2,32,12,128]{3,1,2,0:T(8,128)S(1)} %reduce_sum.27), channel_id=3, replica_groups=mesh['group'=2,'ha_0'=8,'ha_1'=2,'wa'=16] {'ha_1'}, dimensions={0}, use_global_device_ids=true | all-gather | bytes 1179648 | tf_op jit(solution)/shard_map/all_gather | solution.py:40
  104.8 1.6 collective-permute-start.1
  107.5 2.3 %collective-permute-done = bf16[2,2,2,8,1536]{4,3,2,1,0:T(8,128)(2,1)S(1)} collective-permute-done((bf16[2,2,2,8,1536]{4,3,2,1,0:T(8,128)(2,1)S(1)}, bf16[2,2,2,8,1536]{4,3,2,1,0:T(8,128)(2,1)S(1)}, u32[]{:S(2)}, u32[]{:S(2)}) %collective-permute-start) | collective-permute-done | bytes 196640 | tf_op jit(solution)/shard_map/ppermute | solution.py:29
  110.2 3.6 %collective-permute-start.2 = (bf16[2,2,12,2,1536]{4,3,2,1,0:T(2,128)(2,1)S(1)}, bf16[2,2,12,2,1536]{4,3,2,1,0:T(2,128)(2,1)S(1)}, u32[]{:S(2)}, u32[]{:S(2)}) collective-permute-start(bf16[2,2,12,2,1536]{4,3,2,1,0:T(2,128)(2,1)S(1)} %get-tuple-element.16), channel_id=1, source_target_pairs={{0,1},{1,2},{2,3},{3,4},{4,5},{5,6},{6,7},{7,8},{8,9},{9,10},{10,1... | collective-permute-start | bytes 884744 | tf_op jit(solution)/shard_map/ppermute | solution.py:29
  113.8 5.5 %collective-permute-start.3 = (bf16[2,2,12,2,1536]{4,3,2,1,0:T(2,128)(2,1)S(1)}, bf16[2,2,12,2,1536]{4,3,2,1,0:T(2,128)(2,1)S(1)}, u32[]{:S(2)}, u32[]{:S(2)}) collective-permute-start(bf16[2,2,12,2,1536]{4,3,2,1,0:T(2,128)(2,1)S(1)} %get-tuple-element.17), channel_id=1, source_target_pairs={{1,0},{2,1},{3,2},{4,3},{5,4},{6,5},{7,6},{8,7},{9,8},{10,9},{11,1... | collective-permute-start | bytes 884744 | tf_op jit(solution)/shard_map/ppermute | solution.py:31
  119.8 4.4 %collective-permute-done.2 = bf16[2,2,12,2,1536]{4,3,2,1,0:T(2,128)(2,1)S(1)} collective-permute-done((bf16[2,2,12,2,1536]{4,3,2,1,0:T(2,128)(2,1)S(1)}, bf16[2,2,12,2,1536]{4,3,2,1,0:T(2,128)(2,1)S(1)}, u32[]{:S(2)}, u32[]{:S(2)}) %collective-permute-start.2) | collective-permute-done | bytes 294944 | tf_op jit(solution)/shard_map/ppermute | solution.py:29
  124.2 5.7 %collective-permute-done.3 = bf16[2,2,12,2,1536]{4,3,2,1,0:T(2,128)(2,1)S(1)} collective-permute-done((bf16[2,2,12,2,1536]{4,3,2,1,0:T(2,128)(2,1)S(1)}, bf16[2,2,12,2,1536]{4,3,2,1,0:T(2,128)(2,1)S(1)}, u32[]{:S(2)}, u32[]{:S(2)}) %collective-permute-start.3) | collective-permute-done | bytes 294944 | tf_op jit(solution)/shard_map/ppermute | solution.py:31
  129.8 1.5 pad_maximum_fusion
  131.5 1.6 reshape_squeeze.9
  137.2 2.5 %copy.96 = f32[288,12,128]{2,1,0:T(8,128)} copy(f32[288,12,128]{2,0,1:T(8,128)S(1)} %multiply_bitcast_fusion) | data formatting | bytes 3538944 | tf_op jit(solution)/shard_map/mul | solution.py:66
  139.7 2.4 %stack.30 = f32[1,2,12,12,1536]{4,3,2,1,0:T(8,128)S(1)} reshape(f32[288,12,128]{2,1,0:T(8,128)} %copy.96) | data formatting | bytes 3538944 | tf_op jit(solution)/shard_map/stack | solution.py:139
  142.1 1.9 convolution_bitcast_fusion
  144.0 2.6 %copy.98 = f32[288,12,128]{2,1,0:T(8,128)} copy(f32[288,12,128]{2,0,1:T(8,128)S(1)} %convolution_bitcast_fusion) | data formatting | bytes 3538944 | tf_op jit(solution)/shard_map/hqk,qhd->khd/transpose | solution.py:54
  146.6 3.2 %stack.31 = f32[1,2,12,12,1536]{4,3,2,1,0:T(8,128)} reshape(f32[288,12,128]{2,1,0:T(8,128)} %copy.98) | data formatting | bytes 3538944 | tf_op jit(solution)/shard_map/stack | solution.py:139
  150.0 1.5 copy-done.1
  152.3 2.0 collective-permute-start.4
  154.2 5.9 %collective-permute-start.5 = (f32[2,2,12,2,1536]{4,3,2,1,0:T(2,128)S(1)}, f32[2,2,12,2,1536]{4,3,2,1,0:T(2,128)S(1)}, u32[]{:S(2)}, u32[]{:S(2)}) collective-permute-start(f32[2,2,12,2,1536]{4,3,2,1,0:T(2,128)S(1)} %get-tuple-element.11), channel_id=1, source_target_pairs={{0,15},{1,0},{2,1},{3,2},{4,3},{5,4},{6,5},{7,6},{8,7},{9,8},{10,9... | collective-permute-start | bytes 1769480 | tf_op jit(solution)/shard_map/ppermute | solution.py:19
  160.2 23.9 %collective-permute-done.4 = f32[2,2,12,2,1536]{4,3,2,1,0:T(2,128)S(1)} collective-permute-done((f32[2,2,12,2,1536]{4,3,2,1,0:T(2,128)S(1)}, f32[2,2,12,2,1536]{4,3,2,1,0:T(2,128)S(1)}, u32[]{:S(2)}, u32[]{:S(2)}) %collective-permute-start.4) | collective-permute-done | bytes 589856 | tf_op jit(solution)/shard_map/ppermute | solution.py:19
  184.0 1.7 collective-permute-done.5
  191.4 3.4 %collective-permute-done.6 = f32[2,2,2,8,1536]{4,3,2,1,0:T(8,128)} collective-permute-done((f32[2,2,2,8,1536]{4,3,2,1,0:T(8,128)}, f32[2,2,2,8,1536]{4,3,2,1,0:T(8,128)}, u32[]{:S(2)}, u32[]{:S(2)}) %collective-permute-start.6) | collective-permute-done | bytes 393248 | tf_op jit(solution)/shard_map/ppermute | solution.py:19
  197.0 9.8 %all-gather.8.cloned.1.call-done = f32[32,32,12,128]{3,1,2,0:T(8,128)} async-done(((f32[2,32,12,128]{3,1,2,0:T(8,128)}), f32[32,32,12,128]{3,1,2,0:T(8,128)}) %all-gather.8.cloned.1.call-update) | async-done | bytes 6291472 | tf_op jit(solution)/shard_map/all_gather | solution.py:40
  206.8 3.5 %reduce_sum.29 = bf16[2,32,12,128]{3,1,2,0:T(8,128)(2,1)S(1)} reduce(f32[16,2,32,12,128]{4,2,3,1,0:T(8,128)} %bitcast.68, f32[]{:T(128)} %constant.32.clone.1), dimensions={0}, to_apply=%region_2.0 | reduce | flops 1474560 | bytes 6488068 | tf_op jit(solution)/shard_map/reduce_sum | solution.py:40
  (73 shorter events, 24.1 us)
Async XLA Ops:
  7.2 4.5 %copy-start = (bf16[32,1536]{1,0:T(8,128)(2,1)S(1)}, bf16[32,1536]{1,0:T(8,128)(2,1)}, u32[]{:S(2)}) copy-start(bf16[32,1536]{1,0:T(8,128)(2,1)} %param.15) | copy-start | bytes 294916
  7.2 5.1 %copy-start.12 = (bf16[32,1536]{1,0:T(8,128)(2,1)S(1)}, bf16[32,1536]{1,0:T(8,128)(2,1)}, u32[]{:S(2)}) copy-start(bf16[32,1536]{1,0:T(8,128)(2,1)} %param.16) | copy-start | bytes 294916
  7.2 91.7 %all-gather.6.cloned.1.call-start = ((), (), s32[]{:S(2)}) async-start(), calls=%async_computation | async-start | bytes 3538944 | tf_op jit(solution)/shard_map/all_gather | solution.py:40
  12.6 0.7 copy-start.10
  14.3 192.5 %all-gather.8.cloned.1.call-start = ((), (), s32[]{:S(2)}) async-start(), calls=%async_computation.1 | async-start | bytes 6684672 | tf_op jit(solution)/shard_map/all_gather | solution.py:40
  98.9 5.6 %copy-start.8 = (bf16[2,8,8,1536]{3,2,1,0:T(8,128)(2,1)S(1)}, bf16[2,8,8,1536]{3,2,1,0:T(8,128)(2,1)}, u32[]{:S(2)}) copy-start(bf16[2,8,8,1536]{3,2,1,0:T(8,128)(2,1)} %param.11) | copy-start | bytes 1179652
  98.9 5.7 %copy-start.9 = (bf16[2,8,8,1536]{3,2,1,0:T(8,128)(2,1)S(1)}, bf16[2,8,8,1536]{3,2,1,0:T(8,128)(2,1)}, u32[]{:S(2)}) copy-start(bf16[2,8,8,1536]{3,2,1,0:T(8,128)(2,1)} %param.10) | copy-start | bytes 1179652
  104.7 5.1 %collective-permute-start = (bf16[2,2,2,8,1536]{4,3,2,1,0:T(8,128)(2,1)S(1)}, bf16[2,2,2,8,1536]{4,3,2,1,0:T(8,128)(2,1)S(1)}, u32[]{:S(2)}, u32[]{:S(2)}) collective-permute-start(bf16[2,2,2,8,1536]{4,3,2,1,0:T(8,128)(2,1)S(1)} %get-tuple-element.20), channel_id=1, source_target_pairs={{0,16},{16,32},{32,48},{48,64},{64,80},{80,96},{96,112},{112,128},... | collective-permute-start | bytes 589832 | tf_op jit(solution)/shard_map/ppermute | solution.py:29
  104.8 5.0 %collective-permute-start.1 = (bf16[2,2,2,8,1536]{4,3,2,1,0:T(8,128)(2,1)S(1)}, bf16[2,2,2,8,1536]{4,3,2,1,0:T(8,128)(2,1)S(1)}, u32[]{:S(2)}, u32[]{:S(2)}) collective-permute-start(bf16[2,2,2,8,1536]{4,3,2,1,0:T(8,128)(2,1)S(1)} %get-tuple-element.21), channel_id=1, source_target_pairs={{16,0},{32,16},{48,32},{64,48},{80,64},{96,80},{112,96},{128,112},... | collective-permute-start | bytes 589832 | tf_op jit(solution)/shard_map/ppermute | solution.py:31
  110.2 14.0 %collective-permute-start.2 = (bf16[2,2,12,2,1536]{4,3,2,1,0:T(2,128)(2,1)S(1)}, bf16[2,2,12,2,1536]{4,3,2,1,0:T(2,128)(2,1)S(1)}, u32[]{:S(2)}, u32[]{:S(2)}) collective-permute-start(bf16[2,2,12,2,1536]{4,3,2,1,0:T(2,128)(2,1)S(1)} %get-tuple-element.16), channel_id=1, source_target_pairs={{0,1},{1,2},{2,3},{3,4},{4,5},{5,6},{6,7},{7,8},{8,9},{9,10},{10,1... | collective-permute-start | bytes 884744 | tf_op jit(solution)/shard_map/ppermute | solution.py:29
  113.8 16.1 %collective-permute-start.3 = (bf16[2,2,12,2,1536]{4,3,2,1,0:T(2,128)(2,1)S(1)}, bf16[2,2,12,2,1536]{4,3,2,1,0:T(2,128)(2,1)S(1)}, u32[]{:S(2)}, u32[]{:S(2)}) collective-permute-start(bf16[2,2,12,2,1536]{4,3,2,1,0:T(2,128)(2,1)S(1)} %get-tuple-element.17), channel_id=1, source_target_pairs={{1,0},{2,1},{3,2},{4,3},{5,4},{6,5},{7,6},{8,7},{9,8},{10,9},{11,1... | collective-permute-start | bytes 884744 | tf_op jit(solution)/shard_map/ppermute | solution.py:31
  133.9 2.2 %copy-start.5 = (bf16[288,12,128]{2,1,0:T(8,128)(2,1)}, bf16[288,12,128]{2,1,0:T(8,128)(2,1)S(1)}, u32[]{:S(2)}) copy-start(bf16[288,12,128]{2,1,0:T(8,128)(2,1)S(1)} %reshape_squeeze.8) | copy-start | bytes 2654212
  133.9 1.7 copy-start.7
  135.6 1.2 copy-start.4
  136.1 1.0 copy-start.2
  149.8 1.7 copy-start.1
  152.3 31.8 %collective-permute-start.4 = (f32[2,2,12,2,1536]{4,3,2,1,0:T(2,128)S(1)}, f32[2,2,12,2,1536]{4,3,2,1,0:T(2,128)S(1)}, u32[]{:S(2)}, u32[]{:S(2)}) collective-permute-start(f32[2,2,12,2,1536]{4,3,2,1,0:T(2,128)S(1)} %get-tuple-element.10), channel_id=1, source_target_pairs={{0,1},{1,2},{2,3},{3,4},{4,5},{5,6},{6,7},{7,8},{8,9},{9,10},{10,1... | collective-permute-start | bytes 1769480 | tf_op jit(solution)/shard_map/ppermute | solution.py:19
  154.2 34.9 %copy-start.3 = (bf16[12,288,128]{2,1,0:T(8,128)(2,1)S(1)}, bf16[12,288,128]{2,1,0:T(8,128)(2,1)}, u32[]{:S(2)}) copy-start(bf16[12,288,128]{2,1,0:T(8,128)(2,1)} %copy-done.2) | copy-start | bytes 2654212
  154.2 34.9 %copy-start.6 = (bf16[288,12,128]{2,1,0:T(8,128)(2,1)S(1)}, bf16[288,12,128]{2,1,0:T(8,128)(2,1)}, u32[]{:S(2)}) copy-start(bf16[288,12,128]{2,1,0:T(8,128)(2,1)} %copy-done.5) | copy-start | bytes 2654212
  154.2 31.4 %collective-permute-start.5 = (f32[2,2,12,2,1536]{4,3,2,1,0:T(2,128)S(1)}, f32[2,2,12,2,1536]{4,3,2,1,0:T(2,128)S(1)}, u32[]{:S(2)}, u32[]{:S(2)}) collective-permute-start(f32[2,2,12,2,1536]{4,3,2,1,0:T(2,128)S(1)} %get-tuple-element.11), channel_id=1, source_target_pairs={{0,15},{1,0},{2,1},{3,2},{4,3},{5,4},{6,5},{7,6},{8,7},{9,8},{10,9... | collective-permute-start | bytes 1769480 | tf_op jit(solution)/shard_map/ppermute | solution.py:19
  186.4 3.3 %copy-start.11 = (bf16[12,128,32]{1,2,0:T(8,128)(2,1)S(1)}, bf16[12,128,32]{1,2,0:T(8,128)(2,1)}, u32[]{:S(2)}) copy-start(bf16[12,128,32]{1,2,0:T(8,128)(2,1)} %copy-done.10) | copy-start | bytes 294916
  187.3 7.5 %collective-permute-start.6 = (f32[2,2,2,8,1536]{4,3,2,1,0:T(8,128)}, f32[2,2,2,8,1536]{4,3,2,1,0:T(8,128)}, u32[]{:S(2)}, u32[]{:S(2)}) collective-permute-start(f32[2,2,2,8,1536]{4,3,2,1,0:T(8,128)} %get-tuple-element.12), channel_id=1, source_target_pairs={{0,16},{16,32},{32,48},{48,64},{64,80},{80,96},{96,112},{112,128},... | collective-permute-start | bytes 1179656 | tf_op jit(solution)/shard_map/ppermute | solution.py:19
  188.6 6.3 %collective-permute-start.7 = (f32[2,2,2,8,1536]{4,3,2,1,0:T(8,128)}, f32[2,2,2,8,1536]{4,3,2,1,0:T(8,128)}, u32[]{:S(2)}, u32[]{:S(2)}) collective-permute-start(f32[2,2,2,8,1536]{4,3,2,1,0:T(8,128)} %get-tuple-element.13), channel_id=1, source_target_pairs={{0,240},{16,0},{32,16},{48,32},{64,48},{80,64},{96,80},{112,96},{1... | collective-permute-start | bytes 1179656 | tf_op jit(solution)/shard_map/ppermute | solution.py:19
Sparse Core Ops, SparseCore 0:
  14.4 84.4 all-gather.5
  104.7 102.0 all-gather.7
